TPU v7x, 32 devices: a whole 2x2x4 slice. The times are simulated.
32 devices in a mesh: expert: 4 (over y, x), dp: 2 (over core), mp: 4 (over z).
Axes of the slice: x: 2, y: 2, z: 4, core: 2. Of those that a mesh axis runs over, the one named last changes fastest.
Arguments:
- tokens: bfloat16 [96, 4096], P(('expert', 'dp'), 'mp'), may hold values from -6 to 6
- routes: int32 [96, 2], P(('expert', 'dp')), may hold values from 0 to 3, all different within a row; in each aligned block of 12 rows (0 to 11, 12 to 23, ...) at most 9 rows name the same one
- router_weight: bfloat16 [4096, 4], P('mp'), may hold values from -0.09375 to 0.09375
- gate_weight: bfloat16 [4, 4096, 16384], P('expert', None, ('dp', 'mp')), may hold values from -0.09375 to 0.09375
- up_weight: bfloat16 [4, 4096, 16384], P('expert', None, ('dp', 'mp')), may hold values from -0.09375 to 0.09375
- down_weight: bfloat16 [4, 16384, 4096], P('expert', ('dp', 'mp')), may hold values from -0.0625 to 0.0625
Outputs:
- mixed: bfloat16 [96, 4096], P(('expert', 'dp'), 'mp')
Inputs may be any that keep to these rules, and one draw needn't show every extreme that they name: `routes`: each row names two different experts; among the 12 rows of one device (aligned blocks) no expert is named more than 9 times, a bound that some block reaches.
All inputs are finite; a program needn't handle non-finite values.
Results may differ from a plain program's by a relative error of at most 0.0049.
Values may be sent and summed in bfloat16 or wider, within the bound.
No kernel may reach another device: no remote copies, remote signals or barrier semaphores. Data moves between devices by JAX's collectives and lax.ppermute only.
A program may use at most 128 MiB of HBM per device.

v0:
```python
import jax
import jax.numpy as jnp
from jax import lax
from jax.sharding import PartitionSpec as P


def per_device(tokens, routes, router_weight, gate_weight, up_weight, down_weight):
    row_count = tokens.shape[0]
    experts = lax.axis_size("expert")
    capacity = max(2, (6 * row_count + 2 * experts - 1) // (2 * experts))
    partial_logits = jnp.dot(tokens, router_weight, preferred_element_type=jnp.float32)
    logits = lax.psum(partial_logits, "mp")
    labels = jnp.arange(experts, dtype=jnp.int32)
    onehot = (routes[:, :, None] == labels).astype(jnp.int32)
    chosen = jnp.sum(onehot.astype(jnp.float32) * logits[:, None, :], axis=2)
    weights = jnp.stack(
        [jax.nn.sigmoid(chosen[:, 0] - chosen[:, 1]), jax.nn.sigmoid(chosen[:, 1] - chosen[:, 0])],
        axis=1,
    )
    flat_hot = onehot.reshape(row_count * 2, experts)
    before = jnp.cumsum(flat_hot, axis=0) - flat_hot
    position = jnp.sum(flat_hot * before, axis=1)
    places = (position[:, None] == jnp.arange(capacity, dtype=jnp.int32)).astype(jnp.float32)
    assign = (flat_hot.astype(jnp.float32)[:, :, None] * places[:, None, :]).reshape(
        row_count, 2, experts, capacity
    )
    select = jnp.sum(assign, axis=1).astype(jnp.bfloat16)
    combine = jnp.sum(assign * weights[:, :, None, None], axis=1).reshape(
        row_count, experts * capacity
    )
    full_rows = lax.all_gather(tokens, "mp", axis=1, tiled=True)
    full_width = full_rows.shape[1]
    buffer = jnp.einsum(
        "tec,td->ecd", select, full_rows, preferred_element_type=jnp.float32
    ).astype(jnp.bfloat16)
    arrived = lax.all_to_all(buffer, "expert", split_axis=0, concat_axis=0, tiled=True)
    inputs = lax.all_gather(
        arrived.reshape(experts * capacity, full_width), "dp", axis=0, tiled=True
    )
    gate_part = jnp.dot(inputs, gate_weight[0], preferred_element_type=jnp.float32)
    up_part = jnp.dot(inputs, up_weight[0], preferred_element_type=jnp.float32)
    hidden = (jax.nn.silu(gate_part) * up_part).astype(jnp.bfloat16)
    summed = lax.psum_scatter(
        jnp.dot(hidden, down_weight[0], preferred_element_type=jnp.float32),
        "dp",
        scatter_dimension=0,
        tiled=True,
    )
    returned = lax.all_to_all(
        summed.reshape(experts, capacity, full_width),
        "expert",
        split_axis=0,
        concat_axis=0,
        tiled=True,
    )
    partial_mix = jnp.dot(
        combine,
        returned.reshape(experts * capacity, full_width),
        precision=lax.Precision.HIGHEST,
        preferred_element_type=jnp.float32,
    )
    mixed_out = lax.psum_scatter(partial_mix, "mp", scatter_dimension=1, tiled=True)
    return mixed_out.astype(jnp.bfloat16)


def solution(mesh):
    return jax.shard_map(
        per_device,
        mesh=mesh,
        in_specs=(
            P(("expert", "dp"), "mp"),
            P(("expert", "dp"), None),
            P("mp", None),
            P("expert", None, ("dp", "mp")),
            P("expert", None, ("dp", "mp")),
            P("expert", ("dp", "mp"), None),
        ),
        out_specs=P(("expert", "dp"), "mp"),
        check_vma=False,
    )
```

profile of v0, /device:TPU:0, one launch (start us, length us, event | category | flops | bytes accessed | tf_op | source)
XLA Modules:
  0.0 128.2 jit_solution(11685603426469671855)
XLA Ops:
  6.5 0.0 copy-start
  6.5 0.0 reduce-scatter.4.cloned.1.call-start
  6.5 0.8 copy.17
  7.3 0.7 convert_convert_fusion
  8.0 0.1 eq.48
  8.1 0.1 fusion.21
  8.2 0.2 select_reduce_fusion
  8.4 0.1 eq.52
  8.5 0.1 copy.18
  8.6 15.3 %all_gather.6 = bf16[12,4096]{1,0:T(8,128)(2,1)S(1)} all-gather(bf16[12,1024]{1,0:T(8,128)(2,1)} %param.6), channel_id=1, replica_groups=mesh['expert'=4,'dp'=2,'mp'=4] {'mp'}, dimensions={1}, use_global_device_ids=true | all-gather | bytes 122880 | tf_op jit(solution)/shard_map/all_gather | solution.py:31
  23.9 0.0 copy-done
  23.9 0.9 fusion.23
  24.8 12.0 %psum.7 = f32[12,4]{0,1:T(4,128)S(1)} all-reduce(f32[12,4]{0,1:T(4,128)S(1)} %fusion.23), channel_id=1, replica_groups=mesh['expert'=4,'dp'=2,'mp'=4] {'mp'}, use_global_device_ids=true, to_apply=%region_2.0 | all-reduce | flops 48 | bytes 384 | tf_op jit(solution)/shard_map/psum | solution.py:12
  36.8 0.7 multiply_reduce_fusion.1
  37.6 0.3 convolution_convert_fusion
  37.8 10.6 %all_to_all.10 = bf16[4,9,4096]{2,1,0:T(8,128)(2,1)S(1)} all-to-all(bf16[4,9,4096]{2,1,0:T(8,128)(2,1)S(1)} %convolution_convert_fusion), channel_id=1, replica_groups=mesh['expert'=4,'dp'=2,'mp'=4] {'expert'}, dimensions={0} | all-to-all | bytes 589824 | tf_op jit(solution)/shard_map/all_to_all | solution.py:36
  48.5 0.1 reshape.62
  48.6 2.3 %all-gather = bf16[2,36,4096]{2,1,0:T(8,128)(2,1)S(1)} all-gather(bf16[1,36,4096]{2,1,0:T(8,128)(2,1)S(1)} %reshape.62), channel_id=1, replica_groups=mesh['expert'=4,'dp'=2,'mp'=4] {'dp'}, dimensions={0}, use_global_device_ids=true | all-gather | bytes 884736 | tf_op jit(solution)/shard_map/all_gather | solution.py:37
  50.9 0.1 reshape.63
  51.0 8.8 %fusion.5 = f32[72,2048]{1,0:T(8,128)S(1)} fusion(bf16[72,4096]{1,0:T(8,128)(2,1)S(1)} %reshape.63, bf16[1,4096,2048]{2,1,0:T(8,128)(2,1)} %param.9), kind=kOutput, calls=%fused_computation.4 | convolution fusion | flops 1207959552 | bytes 17956864 | tf_op jit(solution)/shard_map/dot_general | solution.py:40
  59.8 0.0 copy-start.1
  59.9 16.6 %fusion.1 = f32[72,4096]{1,0:T(8,128)S(1)} fusion(bf16[1,2048,4096]{2,1,0:T(8,128)(2,1)} %param.11, bf16[72,4096]{1,0:T(8,128)(2,1)S(1)} %reshape.63, bf16[1,4096,2048]{2,1,0:T(8,128)(2,1)} %param.10, f32[72,2048]{1,0:T(8,128)S(1)} %fusion.5), kind=kOutput, calls=%fused_computation | convolution fusion | flops 2416803840 | bytes 35913728 | tf_op jit(solution)/shard_map/dot_general | solution.py:44
  76.4 4.1 %fusion = f32[40,4096]{1,0:T(8,128)S(1)} fusion(f32[72,4096]{1,0:T(8,128)S(1)} %fusion.1), kind=kCustom, calls=%all-reduce-scatter | all-reduce-scatter fusion | flops 327681 | bytes 1835520
  80.6 2.3 %collective-permute-start = (f32[4,4096]{1,0:T(4,128)S(1)}, f32[4,4096]{1,0:T(4,128)S(1)}, u32[]{:S(2)}, u32[]{:S(2)}) collective-permute-start(f32[4,4096]{1,0:T(4,128)S(1)} %slice.10), channel_id=1, source_target_pairs={{0,4},{1,5},{2,6},{3,7},{8,12},{9,13},{10,14},{11,15},{16,20},{17,... | collective-permute-start | bytes 196616
  82.9 0.0 copy-done.1
  82.9 0.6 dynamic-slice.4
  84.1 0.0 collective-permute-done
  84.2 0.4 concatenate
  84.6 0.1 constant_dynamic-slice_fusion
  84.6 0.1 reshape.61
  84.7 17.0 %all_to_all.11 = f32[4,9,4096]{2,1,0:T(8,128)S(1)} all-to-all(f32[4,9,4096]{2,1,0:T(8,128)S(1)} %reshape.61), channel_id=1, replica_groups=mesh['expert'=4,'dp'=2,'mp'=4] {'expert'}, dimensions={0} | all-to-all | bytes 1179648 | tf_op jit(solution)/shard_map/all_to_all | solution.py:49
  101.7 1.3 %convolution_bitcast_fusion = f32[12,4096]{1,0:T(8,128)} fusion(f32[4,9,4096]{2,1,0:T(8,128)S(1)} %all_to_all.11, f32[12,4,9]{0,1,2:T(4,128)S(1)} %get-tuple-element.5), kind=kOutput, calls=%fused_computation.7 | convolution fusion | flops 21233664 | bytes 788160 | tf_op jit(solution)/shard_map/dot_general | solution.py:56
  103.0 0.0 reduce-scatter.4.cloned.1.call-update
  103.1 16.8 %reduce-scatter.4.cloned.1.call-done = f32[12,1024]{1,0:T(8,128)} async-done(((f32[12,4096]{1,0:T(8,128)}), f32[12,1024]{1,0:T(8,128)}) %reduce-scatter.4.cloned.1.call-update) | async-done | bytes 49168 | tf_op jit(solution)/shard_map/reduce_scatter | solution.py:62
  119.9 1.5 %convert_element_type.44 = bf16[12,1024]{1,0:T(8,128)(2,1)} convert(f32[12,1024]{1,0:T(8,128)} %reduce-scatter.4.cloned.1.call-done) | non-fusion elementwise | flops 12288 | bytes 73728 | tf_op jit(solution)/shard_map/convert_element_type | solution.py:63
  (6 shorter events, 0.1 us)
Async XLA Ops:
  6.5 17.3 %copy-start = (bf16[1024,4]{0,1:T(4,128)(2,1)S(1)}, bf16[1024,4]{0,1:T(4,128)(2,1)}, u32[]{:S(2)}) copy-start(bf16[1024,4]{0,1:T(4,128)(2,1)} %param.8) | copy-start | bytes 24580
  6.5 113.4 %reduce-scatter.4.cloned.1.call-start = ((), (), s32[]{:S(2)}) async-start(), calls=%async_computation.3 | async-start | bytes 327680 | tf_op jit(solution)/shard_map/reduce_scatter | solution.py:62
  59.8 23.1 %copy-start.1 = (u32[32]{0:T(128)S(1)}, u32[32]{0:T(128)}, u32[]{:S(2)}) copy-start(u32[32]{0:T(128)} %constant.19) | copy-start | bytes 388
  80.6 3.5 %collective-permute-start = (f32[4,4096]{1,0:T(4,128)S(1)}, f32[4,4096]{1,0:T(4,128)S(1)}, u32[]{:S(2)}, u32[]{:S(2)}) collective-permute-start(f32[4,4096]{1,0:T(4,128)S(1)} %slice.10), channel_id=1, source_target_pairs={{0,4},{1,5},{2,6},{3,7},{8,12},{9,13},{10,14},{11,15},{16,20},{17,... | collective-permute-start | bytes 196616
Sparse Core Ops, SparseCore 0:
  103.2 16.6 reduce-scatter.3
where the time goes:
time: 129 us; the launch traced here: 128 us
  blocking collectives  61.4 us (48%)
  matrix products  27.9 us (22%)
  waiting for transfers between devices  16.9 us (13%)
  between operations  14.2 us (11%)
  other arithmetic  3.21 us (2%)
  local copies, waits for them, and re-layouts  2.45 us (2%)
  starting transfers between devices  2.28 us (2%)
    all_to_all x1, blocking collectives, per_device(): lax.all_to_all(summed.reshape(experts, capacity, full_width), 'expert', s...  17 us
    reduce_scatter x1, waiting for transfers between devices, per_device(): lax.psum_scatter(partial_mix, 'mp', scatter_dimension=1, tiled=True)  16.8 us
    dot_general x1, matrix products, per_device(): jnp.dot(hidden, down_weight[0], preferred_element_type=jnp.float32)  16.6 us
    all_gather x1, blocking collectives, per_device(): full_rows = lax.all_gather(tokens, 'mp', axis=1, tiled=True)  15.3 us
    psum x1, blocking collectives, per_device(): logits = lax.psum(partial_logits, 'mp')  12 us
    all_to_all x1, blocking collectives, per_device(): lax.all_to_all(buffer, 'expert', split_axis=0, concat_axis=0, tiled=True)  10.6 us
    dot_general x1, matrix products, per_device(): jnp.dot(inputs, gate_weight[0], preferred_element_type=jnp.float32)  8.83 us
    unnamed x1, blocking collectives  4.14 us
  transfers between devices with their start and end apart: 2, of which 1 were waited for; matrix products, arithmetic and copies ran while one was open for 0% of the time, Pallas kernels for 0%

commit v1 on v0

--- a/solution.py
+++ b/solution.py
@@ -5,11 +5,19 @@
 
 
 def per_device(tokens, routes, router_weight, gate_weight, up_weight, down_weight):
+
+    def time_the_layers_all(piece_in):
+        p_next = piece_in
+        lanes = lax.axis_size("mp")
+        for ix in [[(dd, dd ^ ii) for dd in range(lanes)] for ii in (1, 2, 4, 8, 16) if ii < lanes]:
+            p_next = p_next + lax.ppermute(p_next, "mp", ix)
+        return p_next
+
     row_count = tokens.shape[0]
     experts = lax.axis_size("expert")
     capacity = max(2, (6 * row_count + 2 * experts - 1) // (2 * experts))
     partial_logits = jnp.dot(tokens, router_weight, preferred_element_type=jnp.float32)
-    logits = lax.psum(partial_logits, "mp")
+    logits = time_the_layers_all(partial_logits)
     labels = jnp.arange(experts, dtype=jnp.int32)
     onehot = (routes[:, :, None] == labels).astype(jnp.int32)
     chosen = jnp.sum(onehot.astype(jnp.float32) * logits[:, None, :], axis=2)

time: 129 us -> 122 us (0.946)
  blocking collectives: 61.4 us -> 47.7 us
  starting transfers between devices: 2.28 us -> 7.99 us
    psum x1 -> x0, blocking collectives: 12 us -> none  [per_device(): logits = lax.psum(partial_logits, 'mp')]
    ppermute x0 -> x2, starting transfers between devices: none -> 5.71 us  [time_the_layers_all(): p_next = p_next + lax.ppermute(p_next, 'mp', ix)]
    all_gather x1, blocking collectives: 15.3 us -> 13.6 us  [per_device(): full_rows = lax.all_gather(tokens, 'mp', axis=1, tiled=True)]
  transfers between devices with their start and end apart: 2 -> 4, of which waited for: 1 -> 1; matrix products, arithmetic and copies ran while one was open for 0% -> 2% of each run, Pallas kernels for 0% -> 0%
where the time goes in v1:
time: 122 us
  blocking collectives  47.7 us (39%)
  matrix products  27.9 us (23%)
  waiting for transfers between devices  17.7 us (15%)
  between operations  14.2 us (12%)
  starting transfers between devices  7.99 us (7%)
  other arithmetic  3.24 us (3%)
  local copies, waits for them, and re-layouts  3.13 us (3%)
    reduce_scatter x1, waiting for transfers between devices, per_device(): lax.psum_scatter(partial_mix, 'mp', scatter_dimension=1, tiled=True)  17.7 us
    all_to_all x1, blocking collectives, per_device(): lax.all_to_all(summed.reshape(experts, capacity, full_width), 'expert', s...  17 us
    dot_general x1, matrix products, per_device(): jnp.dot(hidden, down_weight[0], preferred_element_type=jnp.float32)  16.6 us
    all_gather x1, blocking collectives, per_device(): full_rows = lax.all_gather(tokens, 'mp', axis=1, tiled=True)  13.6 us
    all_to_all x1, blocking collectives, per_device(): lax.all_to_all(buffer, 'expert', split_axis=0, concat_axis=0, tiled=True)  10.6 us
    dot_general x1, matrix products, per_device(): jnp.dot(inputs, gate_weight[0], preferred_element_type=jnp.float32)  8.83 us
    ppermute x2, starting transfers between devices, time_the_layers_all(): p_next = p_next + lax.ppermute(p_next, 'mp', ix)  5.71 us
    unnamed x1, blocking collectives  4.14 us
  transfers between devices with their start and end apart: 4, of which 1 were waited for; matrix products, arithmetic and copies ran while one was open for 2% of the time, Pallas kernels for 0%

profile of v1, /device:TPU:0, one launch (start us, length us, event | category | flops | bytes accessed | tf_op | source)
XLA Modules:
  0.0 121.8 jit_solution(9032143782555172413)
XLA Ops:
  6.5 0.0 copy-start
  6.5 0.0 reduce-scatter.4.cloned.1.call-start
  6.5 0.7 copy-done
  7.2 0.9 fusion.23
  8.1 3.1 %collective-permute-start = (f32[12,4]{0,1:T(4,128)S(1)}, f32[12,4]{0,1:T(4,128)S(1)}, u32[]{:S(2)}, u32[]{:S(2)}) collective-permute-start(f32[12,4]{0,1:T(4,128)S(1)} %fusion.23), channel_id=1, source_target_pairs={{0,1},{1,0},{2,3},{3,2},{4,5},{5,4},{6,7},{7,6},{8,9},{9,8},{10,11... | collective-permute-start | bytes 584 | tf_op jit(solution)/shard_map/ppermute | solution.py:13
  11.2 0.8 copy.17
  11.9 0.1 eq.48
  12.0 0.1 fusion.21
  12.1 0.2 select_reduce_fusion
  12.3 0.1 eq.52
  12.4 0.1 copy.18
  12.5 0.7 convert_convert_fusion
  13.2 0.0 collective-permute-done
  13.2 2.7 %collective-permute-start.1 = (f32[12,4]{0,1:T(4,128)S(1)}, f32[12,4]{0,1:T(4,128)S(1)}, u32[]{:S(2)}, u32[]{:S(2)}) collective-permute-start(f32[12,4]{0,1:T(4,128)S(1)} %add.22), channel_id=1, source_target_pairs={{0,2},{1,3},{2,0},{3,1},{4,6},{5,7},{6,4},{7,5},{8,10},{9,11},{10,... | collective-permute-start | bytes 584 | tf_op jit(solution)/shard_map/ppermute | solution.py:13
  15.9 13.6 %all_gather.6 = bf16[12,4096]{1,0:T(8,128)(2,1)S(1)} all-gather(bf16[12,1024]{1,0:T(8,128)(2,1)} %param.6), channel_id=1, replica_groups=mesh['expert'=4,'dp'=2,'mp'=4] {'mp'}, dimensions={1}, use_global_device_ids=true | all-gather | bytes 122880 | tf_op jit(solution)/shard_map/all_gather | solution.py:39
  29.5 0.0 collective-permute-done.1
  29.5 0.7 multiply_reduce_fusion.1
  30.3 0.3 convolution_convert_fusion
  30.6 10.6 %all_to_all.10 = bf16[4,9,4096]{2,1,0:T(8,128)(2,1)S(1)} all-to-all(bf16[4,9,4096]{2,1,0:T(8,128)(2,1)S(1)} %convolution_convert_fusion), channel_id=1, replica_groups=mesh['expert'=4,'dp'=2,'mp'=4] {'expert'}, dimensions={0} | all-to-all | bytes 589824 | tf_op jit(solution)/shard_map/all_to_all | solution.py:44
  41.2 0.1 reshape.62
  41.3 2.3 %all-gather = bf16[2,36,4096]{2,1,0:T(8,128)(2,1)S(1)} all-gather(bf16[1,36,4096]{2,1,0:T(8,128)(2,1)S(1)} %reshape.62), channel_id=1, replica_groups=mesh['expert'=4,'dp'=2,'mp'=4] {'dp'}, dimensions={0}, use_global_device_ids=true | all-gather | bytes 884736 | tf_op jit(solution)/shard_map/all_gather | solution.py:45
  43.6 0.1 reshape.63
  43.7 8.8 %fusion.5 = f32[72,2048]{1,0:T(8,128)S(1)} fusion(bf16[72,4096]{1,0:T(8,128)(2,1)S(1)} %reshape.63, bf16[1,4096,2048]{2,1,0:T(8,128)(2,1)} %param.9), kind=kOutput, calls=%fused_computation.4 | convolution fusion | flops 1207959552 | bytes 17956864 | tf_op jit(solution)/shard_map/dot_general | solution.py:48
  52.6 0.0 copy-start.1
  52.6 16.6 %fusion.1 = f32[72,4096]{1,0:T(8,128)S(1)} fusion(bf16[1,2048,4096]{2,1,0:T(8,128)(2,1)} %param.11, bf16[72,4096]{1,0:T(8,128)(2,1)S(1)} %reshape.63, bf16[1,4096,2048]{2,1,0:T(8,128)(2,1)} %param.10, f32[72,2048]{1,0:T(8,128)S(1)} %fusion.5), kind=kOutput, calls=%fused_computation | convolution fusion | flops 2416803840 | bytes 35913728 | tf_op jit(solution)/shard_map/dot_general | solution.py:52
  69.2 4.1 %fusion = f32[40,4096]{1,0:T(8,128)S(1)} fusion(f32[72,4096]{1,0:T(8,128)S(1)} %fusion.1), kind=kCustom, calls=%all-reduce-scatter | all-reduce-scatter fusion | flops 327681 | bytes 1835520
  73.3 2.3 %collective-permute-start.2 = (f32[4,4096]{1,0:T(4,128)S(1)}, f32[4,4096]{1,0:T(4,128)S(1)}, u32[]{:S(2)}, u32[]{:S(2)}) collective-permute-start(f32[4,4096]{1,0:T(4,128)S(1)} %slice.10), channel_id=1, source_target_pairs={{0,4},{1,5},{2,6},{3,7},{8,12},{9,13},{10,14},{11,15},{16,20},{17,... | collective-permute-start | bytes 196616
  75.6 0.0 copy-done.1
  75.6 0.6 dynamic-slice.4
  76.9 0.0 collective-permute-done.2
  76.9 0.4 concatenate
  77.3 0.1 constant_dynamic-slice_fusion
  77.4 0.1 reshape.61
  77.5 17.0 %all_to_all.11 = f32[4,9,4096]{2,1,0:T(8,128)S(1)} all-to-all(f32[4,9,4096]{2,1,0:T(8,128)S(1)} %reshape.61), channel_id=1, replica_groups=mesh['expert'=4,'dp'=2,'mp'=4] {'expert'}, dimensions={0} | all-to-all | bytes 1179648 | tf_op jit(solution)/shard_map/all_to_all | solution.py:57
  94.5 1.3 %convolution_bitcast_fusion = f32[12,4096]{1,0:T(8,128)} fusion(f32[4,9,4096]{2,1,0:T(8,128)S(1)} %all_to_all.11, f32[12,4,9]{0,1,2:T(4,128)S(1)} %get-tuple-element.5), kind=kOutput, calls=%fused_computation.7 | convolution fusion | flops 21233664 | bytes 788160 | tf_op jit(solution)/shard_map/dot_general | solution.py:64
  95.8 0.0 reduce-scatter.4.cloned.1.call-update
  95.8 17.7 %reduce-scatter.4.cloned.1.call-done = f32[12,1024]{1,0:T(8,128)} async-done(((f32[12,4096]{1,0:T(8,128)}), f32[12,1024]{1,0:T(8,128)}) %reduce-scatter.4.cloned.1.call-update) | async-done | bytes 49168 | tf_op jit(solution)/shard_map/reduce_scatter | solution.py:70
  113.5 1.5 %convert_element_type.44 = bf16[12,1024]{1,0:T(8,128)(2,1)} convert(f32[12,1024]{1,0:T(8,128)} %reduce-scatter.4.cloned.1.call-done) | non-fusion elementwise | flops 12288 | bytes 73728 | tf_op jit(solution)/shard_map/convert_element_type | solution.py:71
  (8 shorter events, 0.1 us)
Async XLA Ops:
  6.5 0.7 copy-start
  6.5 107.0 %reduce-scatter.4.cloned.1.call-start = ((), (), s32[]{:S(2)}) async-start(), calls=%async_computation.3 | async-start | bytes 327680 | tf_op jit(solution)/shard_map/reduce_scatter | solution.py:70
  8.1 5.1 %collective-permute-start = (f32[12,4]{0,1:T(4,128)S(1)}, f32[12,4]{0,1:T(4,128)S(1)}, u32[]{:S(2)}, u32[]{:S(2)}) collective-permute-start(f32[12,4]{0,1:T(4,128)S(1)} %fusion.23), channel_id=1, source_target_pairs={{0,1},{1,0},{2,3},{3,2},{4,5},{5,4},{6,7},{7,6},{8,9},{9,8},{10,11... | collective-permute-start | bytes 584 | tf_op jit(solution)/shard_map/ppermute | solution.py:13
  13.2 16.3 %collective-permute-start.1 = (f32[12,4]{0,1:T(4,128)S(1)}, f32[12,4]{0,1:T(4,128)S(1)}, u32[]{:S(2)}, u32[]{:S(2)}) collective-permute-start(f32[12,4]{0,1:T(4,128)S(1)} %add.22), channel_id=1, source_target_pairs={{0,2},{1,3},{2,0},{3,1},{4,6},{5,7},{6,4},{7,5},{8,10},{9,11},{10,... | collective-permute-start | bytes 584 | tf_op jit(solution)/shard_map/ppermute | solution.py:13
  52.6 23.1 %copy-start.1 = (u32[32]{0:T(128)S(1)}, u32[32]{0:T(128)}, u32[]{:S(2)}) copy-start(u32[32]{0:T(128)} %constant.19) | copy-start | bytes 388
  73.3 3.5 %collective-permute-start.2 = (f32[4,4096]{1,0:T(4,128)S(1)}, f32[4,4096]{1,0:T(4,128)S(1)}, u32[]{:S(2)}, u32[]{:S(2)}) collective-permute-start(f32[4,4096]{1,0:T(4,128)S(1)} %slice.10), channel_id=1, source_target_pairs={{0,4},{1,5},{2,6},{3,7},{8,12},{9,13},{10,14},{11,15},{16,20},{17,... | collective-permute-start | bytes 196616
Sparse Core Ops, SparseCore 0:
  95.9 17.5 reduce-scatter.3
